TPU v7x, 32 devices: a whole 2x2x4 slice. The times are simulated.
32 devices in a mesh: groups: 2 (over x), tok: 16 (over z, y, core).
Axes of the slice: x: 2, y: 2, z: 4, core: 2. Of those that a mesh axis runs over, the one named last changes fastest.
Arguments:
- activations: bfloat16 [32, 128, 768], P(('groups', 'tok')), parts along dimension 0, may hold values from -32 to 32
- pair_repr: bfloat16 [256, 128, 128], P('groups', 'tok'), parts along dimension 0, may hold values from -6 to 6
- pair_gain: float32 [128], replicated, may hold values from 0.5 to 1.5
- bias_weight: float32 [128, 16], replicated, may hold values from -0.5 to 0.5
- proj_weight: bfloat16 [768, 3072], replicated, may hold values from -0.21875 to 0.21875
- query_bias: float32 [768], replicated, may hold values from -5 to 5
- out_weight: bfloat16 [768, 768], replicated, may hold values from -0.21875 to 0.21875
- token_mask: int32 [256], P('groups'), parts along dimension 0, may hold values 0 or 1
- out_cotangent: bfloat16 [32, 128, 768], P(('groups', 'tok')), parts along dimension 0, may hold values from -6 to 6
Outputs:
- grad_activations: bfloat16 [32, 128, 768], P(('groups', 'tok')), parts along dimension 0
- grad_pair: bfloat16 [256, 128, 128], P('groups', 'tok'), parts along dimension 0
- grad_proj: float32 [1536, 3072], P(('groups', 'tok')), parts along dimension 0
- grad_out_weight: float32 [1536, 768], P(('groups', 'tok')), parts along dimension 0
- grad_query_bias: float32 [1536], P('groups'), parts along dimension 0
- grad_bias_weight: float32 [256, 16], P('groups'), parts along dimension 0
- grad_pair_gain: float32 [256], P('groups'), parts along dimension 0
There are 2 independent parts, one for each index of `groups`. A program takes and returns all parts, laid end to end along the dimension named above; an argument that names none is the same for every part. Nothing has to cross between parts.
All inputs are finite; a program needn't handle non-finite values.
Results may differ from a plain program's by a relative error of at most 0.015.
The roundings to bfloat16 on the way count: a program that leaves them out, or rounds other values in their place, can miss the bound.
Values may be sent and summed in bfloat16 or wider, within the bound.
A program may use at most 128 MiB of HBM per device.

v0:
```python
import math
import jax
import jax.numpy as jnp
from jax import lax
from jax.sharding import PartitionSpec as P

HEADS = 16
HD = 48
EPSILON = 1e-05
MASK_PENALTY = 10000.0


def as_sent(value):
    return jax.tree.map(lambda a: a.astype(jnp.bfloat16) if a.dtype == jnp.float32 else a, value)


def partner(block, axis, apart):
    count = lax.axis_size(axis)
    route = []
    for low in range(count):
        high = low | 1 << apart
        if high != low and high < count:
            route += [(low, high), (high, low)]
    return lax.ppermute(block, axis, route)


def dest_order(tensor):
    return tensor.reshape((tensor.shape[0] * tensor.shape[1],) + tensor.shape[2:])


def source_heads(tensor, blocks):
    rest = tensor.shape[1:]
    return tensor.reshape((HEADS, blocks) + rest)


def row_blocks(tensor, blocks):
    channels = tensor.shape[0]
    block_rows = tensor.shape[3] // blocks
    shaped = tensor.reshape(channels, HEADS, HD, blocks, block_rows)
    return dest_order(shaped.transpose(1, 3, 0, 2, 4))


def token_rows(tensor, blocks):
    shaped = source_heads(tensor, blocks)
    channels = shaped.shape[2]
    block_rows = shaped.shape[4]
    return shaped.transpose(1, 4, 2, 0, 3).reshape(blocks * block_rows, channels * HEADS * HD)


def grouped(tree, group_size):
    return tree.reshape((tree.shape[0] // group_size, group_size) + tree.shape[1:])


def ungrouped(tree):
    return tree.reshape((tree.shape[0] * tree.shape[1],) + tree.shape[2:])


def xor_order(array, position, bit_count):
    for level in range(bit_count):
        shaped = array.reshape((array.shape[0] // (2 << level), 2, 1 << level) + array.shape[1:])
        bit_set = position // (1 << level) % 2
        array = jnp.where(bit_set == 1, shaped[:, ::-1], shaped).reshape(array.shape)
    return array


def group_regroup(array, position, bit_count, offset):
    holding = xor_order(array, position, bit_count)
    for level in range(bit_count):
        shaped = holding.reshape(
            (holding.shape[0] // (2 << level), 2, 1 << level) + holding.shape[1:]
        )
        arrived_half = partner(as_sent(shaped[:, 1]), "tok", offset + level)
        holding = jnp.stack([shaped[:, 0], arrived_half], axis=1).reshape(holding.shape)
    return xor_order(holding, position, bit_count)


def probabilities(query, keys, bias_full, key_bias):
    scores = jnp.einsum("di,dj->ij", query, keys, preferred_element_type=jnp.float32) * HD ** (-0.5)
    scores = scores + bias_full + key_bias[None, :]
    peak = jnp.max(scores, axis=1, keepdims=True)
    expo = jnp.exp(scores - peak)
    return expo / jnp.sum(expo, axis=1, keepdims=True)


def attend_forward(values, probs):
    return jnp.einsum(
        "dj,ij->di", values, probs.astype(jnp.bfloat16), preferred_element_type=jnp.float32
    ).astype(jnp.bfloat16)


def gate_terms(grad_gated, gate, attended):
    gate32 = gate.astype(jnp.float32)
    grad32 = grad_gated.astype(jnp.float32)
    att32 = attended.astype(jnp.float32)
    gated = (gate32 * att32).astype(jnp.bfloat16)
    grad_att = (grad32 * gate32).astype(jnp.bfloat16)
    grad_logit = (grad32 * att32 * gate32 * (1.0 - gate32)).astype(jnp.bfloat16)
    return (grad_att, grad_logit, gated)


def attend_back(query, keys, values, probs, grad_att):
    rounded = probs.astype(jnp.bfloat16)
    grad_value = jnp.einsum("di,ij->dj", grad_att, rounded, preferred_element_type=jnp.float32)
    grad_probs = jnp.einsum("di,dj->ij", grad_att, values, preferred_element_type=jnp.float32)
    grad_scores = probs * (grad_probs - jnp.sum(probs * grad_probs, axis=1, keepdims=True))
    scores_b = grad_scores.astype(jnp.bfloat16)
    grad_query = jnp.einsum(
        "ij,dj->di", scores_b, keys, preferred_element_type=jnp.float32
    ) * HD ** (-0.5)
    grad_key = jnp.einsum(
        "ij,di->dj", scores_b, query, preferred_element_type=jnp.float32
    ) * HD ** (-0.5)
    return (grad_query.astype(jnp.bfloat16), jnp.stack([grad_key, grad_value], axis=0), grad_scores)


def make_joint(bias_full, key_bias):

    def joint_one(front, kv_one):
        probs = probabilities(front[0], kv_one[0], bias_full, key_bias)
        attended_one = attend_forward(kv_one[1], probs)
        grad_att, grad_logit, gated_one = gate_terms(front[2], front[1], attended_one)
        grad_query, grad_kv, grad_scores = attend_back(
            front[0], kv_one[0], kv_one[1], probs, grad_att
        )
        return (jnp.stack([grad_query, grad_logit, gated_one], axis=0), grad_kv, grad_scores)

    return joint_one


def on_device(
    activations,
    pair_repr,
    pair_gain,
    bias_weight,
    proj_weight,
    query_bias,
    out_weight,
    token_mask,
    out_cotangent,
):
    tok_count = lax.axis_size("tok")
    blocks = tok_count // HEADS
    all_tokens = activations.shape[1]
    feature = activations.shape[2]
    block_rows = all_tokens // blocks
    bit_count = blocks.bit_length() - 1
    position = lax.axis_index("tok") % blocks
    offset = 0
    act_rows = activations.reshape(all_tokens, feature)
    cot_rows = out_cotangent.reshape(all_tokens, feature)
    proj = jnp.dot(act_rows, proj_weight, preferred_element_type=jnp.float32)
    shift = jnp.concatenate([query_bias, jnp.zeros((2 * feature,), jnp.float32)])
    qkv_rows = (proj[:, : 3 * feature] + shift[None, :]).astype(jnp.bfloat16)
    gate = jax.nn.sigmoid(proj[:, 3 * feature :]).astype(jnp.bfloat16)
    grad_gated = jnp.einsum(
        "rn,mn->rm", cot_rows, out_weight, preferred_element_type=jnp.float32
    ).astype(jnp.bfloat16)
    pair_f = pair_repr.astype(jnp.float32)
    mean_z = jnp.mean(pair_f, axis=-1, keepdims=True)
    centred = pair_f - mean_z
    rstd = lax.rsqrt(jnp.mean(centred * centred, axis=-1, keepdims=True) + EPSILON)
    normed = centred * rstd
    scaled = normed * pair_gain
    bias_cols = jnp.einsum(
        "ijc,ch->hij", scaled, bias_weight, precision=lax.Precision.HIGHEST
    ).astype(jnp.bfloat16)
    key_bias = (token_mask.astype(jnp.float32) - 1.0) * MASK_PENALTY
    joint_rows = jnp.concatenate([qkv_rows[:, :feature], gate, grad_gated], axis=1)
    bias_wide = jnp.broadcast_to(bias_cols[:, None], (HEADS, blocks) + bias_cols.shape[1:])
    bias_full = lax.all_to_all(
        dest_order(bias_wide), "tok", split_axis=0, concat_axis=2, tiled=True
    )[0].astype(jnp.float32)
    per_item = make_joint(bias_full, key_bias)
    five_rows = jnp.concatenate([joint_rows, qkv_rows[:, feature:]], axis=1)
    five_view = five_rows.reshape(all_tokens, 5, HEADS, HD).transpose(1, 2, 3, 0)
    arrived = lax.all_to_all(
        row_blocks(five_view, blocks), "tok", split_axis=0, concat_axis=0, tiled=True
    )
    regrouped = group_regroup(
        arrived.reshape((blocks, HEADS) + arrived.shape[1:]), position, bit_count, offset
    )
    head_items = regrouped.transpose(1, 2, 3, 0, 4).reshape(HEADS, 5, HD, all_tokens)
    group_size = math.gcd(HEADS, max(1, 512 // all_tokens))

    def sample_step(total, pieces):
        merged, grad_kv, grad_scores = jax.vmap(per_item)(pieces[:, :3], pieces[:, 3:])
        results = jnp.concatenate([merged, grad_kv.astype(jnp.bfloat16)], axis=1)
        return (total + jnp.sum(grad_scores, axis=0), results)

    start_total = jnp.zeros((all_tokens, all_tokens), jnp.float32)
    grad_bias_part, results = lax.scan(sample_step, start_total, grouped(head_items, group_size))
    results = ungrouped(results)
    outgoing = results.reshape(HEADS, 5, HD, blocks, block_rows).transpose(3, 0, 1, 2, 4)
    returned = group_regroup(outgoing, position, bit_count, offset).reshape(
        tok_count, 5, HD, block_rows
    )
    came_back = lax.all_to_all(returned, "tok", split_axis=0, concat_axis=0, tiled=True)
    rows_back = token_rows(came_back, blocks)
    grad_rows = jnp.concatenate(
        [rows_back[:, :feature], rows_back[:, 3 * feature :], rows_back[:, feature : 2 * feature]],
        axis=1,
    )
    gated = rows_back[:, 2 * feature : 3 * feature]
    received = lax.all_to_all(
        grad_bias_part[None].astype(jnp.bfloat16), "tok", split_axis=2, concat_axis=0, tiled=True
    ).astype(jnp.float32)
    grad_bias = jnp.sum(source_heads(received, blocks), axis=1)
    first = jnp.einsum("rc,rn->cn", act_rows, grad_rows, preferred_element_type=jnp.float32)
    second = jnp.einsum("rc,rn->cn", gated, cot_rows, preferred_element_type=jnp.float32)
    weight_grads = lax.psum_scatter(
        jnp.concatenate([first, second], axis=1), "tok", scatter_dimension=0, tiled=True
    )
    grad_activations = jnp.einsum(
        "rn,dn->rd", grad_rows, proj_weight, preferred_element_type=jnp.float32
    ).astype(jnp.bfloat16)
    grad_zg = jnp.einsum("hij,ch->ijc", grad_bias, bias_weight, precision=lax.Precision.HIGHEST)
    weight_part = jnp.einsum("ijc,hij->ch", scaled, grad_bias, precision=lax.Precision.HIGHEST)
    gain_part = jnp.sum(normed * grad_zg, axis=(0, 1))
    query_part = jnp.sum(grad_rows[:, :feature].astype(jnp.float32), axis=0)
    grad_query_bias, grad_bias_weight, grad_pair_gain = lax.psum(
        (query_part, weight_part, gain_part), "tok"
    )
    grad_norm = grad_zg * pair_gain
    grad_pair = (
        grad_norm
        - jnp.mean(grad_norm, axis=-1, keepdims=True)
        - normed * jnp.mean(grad_norm * normed, axis=-1, keepdims=True)
    ) * rstd
    return (
        grad_activations.reshape(1, all_tokens, feature),
        grad_pair.astype(jnp.bfloat16),
        weight_grads[:, : 4 * feature],
        weight_grads[:, 4 * feature :],
        grad_query_bias,
        grad_bias_weight,
        grad_pair_gain,
    )


def solution(mesh):
    in_specs = (
        P(("groups", "tok"), None, None),
        P("groups", "tok", None),
        P(),
        P(),
        P(),
        P(),
        P(),
        P("groups"),
        P(("groups", "tok"), None, None),
    )
    out_specs = (
        P(("groups", "tok"), None, None),
        P("groups", "tok", None),
        P(("groups", "tok"), None),
        P(("groups", "tok"), None),
        P("groups"),
        P("groups", None),
        P("groups"),
    )
    return jax.shard_map(
        on_device, mesh=mesh, in_specs=in_specs, out_specs=out_specs, check_vma=False
    )
```

profile of v0, /device:TPU:0, one launch (start us, length us, event | category | flops | bytes accessed | tf_op | source)
XLA Modules:
  0.0 252.7 jit_solution(9659718730812204163)
XLA Ops:
  7.2 1.2 copy.67
  8.6 1.2 fusion.28
  9.8 0.6 copy.69
  10.4 7.4 %all-to-all-start.1 = ((bf16[16,128,8]{1,2,0:T(8,128)(2,1)}), bf16[16,128,8]{1,2,0:T(8,128)(2,1)S(1)}, u32[]{:S(2)}, u32[]{:S(2)}) async-start(bf16[16,128,8]{1,2,0:T(8,128)(2,1)} %copy.69), calls=%async_computation.1 | async-start | bytes 65536 | tf_op jit(solution)/shard_map/all_to_all | solution.py:170
  17.9 3.2 %fusion.58 = f32[128,3072]{1,0:T(8,128)S(1)} fusion(bf16[768,3072]{1,0:T(8,128)(2,1)} %param.15, bf16[1,128,768]{2,1,0:T(8,128)(2,1)} %param.11), kind=kOutput, calls=%fused_computation.93 | convolution fusion | flops 603979776 | bytes 6488064 | tf_op jit(solution)/shard_map/dot_general | solution.py:151
  21.4 0.6 copy-done.1
  22.0 0.5 convolution_convert_fusion.3
  22.7 0.7 copy.65
  23.3 1.0 copy.66
  24.5 5.9 %all-to-all-start = ((bf16[16,5,48,128]{3,2,1,0:T(8,128)(2,1)}), bf16[16,5,48,128]{3,2,1,0:T(8,128)(2,1)S(1)}, u32[]{:S(2)}, u32[]{:S(2)}) async-start(bf16[16,5,48,128]{3,2,1,0:T(8,128)(2,1)} %copy.66), calls=%async_computation | async-start | bytes 1966080 | tf_op jit(solution)/shard_map/all_to_all | solution.py:176
  30.5 21.7 %all-to-all-done = bf16[16,5,48,128]{3,2,1,0:T(8,128)(2,1)S(1)} async-done(((bf16[16,5,48,128]{3,2,1,0:T(8,128)(2,1)}), bf16[16,5,48,128]{3,2,1,0:T(8,128)(2,1)S(1)}, u32[]{:S(2)}, u32[]{:S(2)}) %all-to-all-start) | async-done | bytes 983072 | tf_op jit(solution)/shard_map/all_to_all | solution.py:176
  52.2 10.9 %while.13 = (s32[]{:T(128)}, f32[128,128]{0,1:T(8,128)S(1)}, bf16[4,4,5,48,128]{4,3,2,1,0:T(8,128)(2,1)}, bf16[4,4,5,48,128]{4,3,2,1,0:T(8,128)(2,1)S(1)}, f32[1...) while((s32[]{:T(128)}, f32[128,128]{0,1:T(8,128)S(1)}, ...), condition=%wide.region_7.8_spmd.clone, body=%wide.region_2.7_spmd.clone.sunk | while | flops 52896640 | bytes 4685423 | solution.py:191
  52.3 0.3 fusion.94
  52.6 0.5 fusion.96
  53.0 0.4 fusion.98
  53.5 0.3 multiply_reduce_fusion.3
  54.2 0.7 copy_dynamic-update-slice_fusion.2
  55.0 0.3 fusion.94
  55.3 0.5 fusion.96
  55.7 0.4 fusion.98
  57.0 0.7 copy_dynamic-update-slice_fusion.2
  57.7 0.3 fusion.94
  58.0 0.5 fusion.96
  58.5 0.4 fusion.98
  58.9 0.3 multiply_reduce_fusion.3
  59.7 0.7 copy_dynamic-update-slice_fusion.2
  60.4 0.3 fusion.94
  60.7 0.5 fusion.96
  61.2 0.4 fusion.98
  61.6 0.3 multiply_reduce_fusion.3
  62.4 0.7 copy_dynamic-update-slice_fusion.2
  63.1 30.0 %all_to_all.34 = bf16[16,5,48,128]{3,2,1,0:T(8,128)(2,1)S(1)} all-to-all(bf16[16,5,48,128]{3,2,1,0:T(8,128)(2,1)} %bitcast.220), channel_id=1, replica_groups=mesh['groups'=2,'tok'=16] {'tok'}, dimensions={0} | all-to-all | bytes 1966080 | tf_op jit(solution)/shard_map/all_to_all | solution.py:197
  93.3 0.8 copy-done.2
  94.0 0.5 fusion.53
  94.6 1.4 convolution_bitcast_fusion
  95.9 4.6 %pad_maximum_fusion = f32[768,3840]{0,1:T(8,128)} fusion(f32[768,768]{0,1:T(8,128)S(1)} %fusion.53, f32[768,3072]{0,1:T(8,128)S(1)} %convolution_bitcast_fusion), kind=kLoop, calls=%fused_computation.49 | loop fusion | flops 2949120 | bytes 23592960 | tf_op jit(solution)/shard_map/concatenate | solution.py:211
  100.6 12.4 %copy.86 = f32[768,3840]{1,0:T(8,128)} copy(f32[768,3840]{0,1:T(8,128)} %pad_maximum_fusion) | data formatting | bytes 23592960
  113.3 0.5 broadcast.94
  113.8 0.8 reduce
  114.6 11.2 %all_to_all.35 = bf16[16,2,512]{2,1,0:T(2,128)(2,1)S(1)} all-to-all(bf16[16,2,512]{2,1,0:T(2,128)(2,1)S(1)} %reshape.98), channel_id=1, replica_groups=mesh['groups'=2,'tok'=16] {'tok'}, dimensions={0} | all-to-all | bytes 65536 | tf_op jit(solution)/shard_map/all_to_all | solution.py:204
  125.9 0.6 fusion.41
  126.7 0.9 copy.77
  127.6 1.2 convolution_bitcast_fusion.1
  129.0 60.7 %all-reduce.1 = (f32[768]{0:T(1024)}, f32[128,16]{0,1:T(8,128)}, f32[128]{0:T(128)}) all-reduce(f32[768]{0:T(1024)S(1)} %convert_reduce_fusion.1, f32[128,16]{0,1:T(8,128)S(1)} %convolution_bitcast_fusion.1, f32[128]{0:T(128)S(1)} %get-tuple-element.109), channel_id=1, replica_groups=mesh['groups'=2,'tok'=16] {'tok'}, use_global_device_ids=true, to_apply=%region_12.13 | all-reduce | flops 2944 | bytes 23552 | tf_op jit(solution)/shard_map/psum | solution.py:220
  189.7 4.7 %fusion.27 = bf16[1,128,768]{2,1,0:T(8,128)(2,1)} fusion(bf16[768,3072]{1,0:T(8,128)(2,1)} %param.15, bf16[128,768]{0,1:T(8,128)(2,1)S(1)} %get-tuple-element.136, bf16[128,1536]{0,1:T(8,128)(2,1)S(1)} %slice.80, bf16[128,768]{0,1:T(8,128)(2,1)S(1)} %get-tuple-element.135), kind=kOutput, calls=%fused_computation.55 | convolution fusion | flops 606437376 | bytes 5701632 | tf_op jit(solution)/shard_map/rn,dn->rd/dot_general | solution.py:213
  194.4 48.0 %reduce-scatter.4.cloned.1.call-done = f32[48,3840]{1,0:T(8,128)} async-done(((f32[768,3840]{1,0:T(8,128)}), f32[48,3840]{1,0:T(8,128)}) %reduce-scatter.4.cloned.1.call-update) | async-done | bytes 737296
  242.4 1.6 slice.84
  244.0 1.9 slice.83
  (73 shorter events, 3.7 us)
Async XLA Ops:
  7.2 14.2 %copy-start = (bf16[768,768]{1,0:T(8,128)(2,1)S(1)}, bf16[768,768]{1,0:T(8,128)(2,1)}, u32[]{:S(2)}) copy-start(bf16[768,768]{1,0:T(8,128)(2,1)} %param.17) | copy-start | bytes 3538948
  10.4 14.1 %all-to-all-start.1 = ((bf16[16,128,8]{1,2,0:T(8,128)(2,1)}), bf16[16,128,8]{1,2,0:T(8,128)(2,1)S(1)}, u32[]{:S(2)}, u32[]{:S(2)}) async-start(bf16[16,128,8]{1,2,0:T(8,128)(2,1)} %copy.69), calls=%async_computation.1 | async-start | bytes 65536 | tf_op jit(solution)/shard_map/all_to_all | solution.py:170
  17.8 3.4 %copy-start.5 = (f32[768]{0:T(1024)S(1)}, f32[768]{0:T(1024)}, u32[]{:S(2)}) copy-start(f32[768]{0:T(1024)} %param.16) | copy-start | bytes 9220
  21.1 0.9 copy-start.1
  23.3 7.2 %copy-start.8 = (s32[128]{0:T(128)S(1)}, s32[128]{0:T(128)}, u32[]{:S(2)}) copy-start(s32[128]{0:T(128)} %param.18) | copy-start | bytes 1540
  24.5 27.8 %all-to-all-start = ((bf16[16,5,48,128]{3,2,1,0:T(8,128)(2,1)}), bf16[16,5,48,128]{3,2,1,0:T(8,128)(2,1)S(1)}, u32[]{:S(2)}, u32[]{:S(2)}) async-start(bf16[16,5,48,128]{3,2,1,0:T(8,128)(2,1)} %copy.66), calls=%async_computation | async-start | bytes 1966080 | tf_op jit(solution)/shard_map/all_to_all | solution.py:176
  30.4 212.0 %reduce-scatter.4.cloned.1.call-start = ((), (), s32[]{:S(2)}) async-start(), calls=%async_computation.5 | async-start | bytes 12533760
  93.1 0.9 copy-start.2
  93.2 1.3 copy-start.3
  113.0 12.9 %copy-start.6 = (f32[128]{0:T(128)S(1)}, f32[128]{0:T(128)}, u32[]{:S(2)}) copy-start(f32[128]{0:T(128)} %param.13) | copy-start | bytes 1540
  113.0 12.9 %copy-start.7 = (f32[128,16]{0,1:T(8,128)S(1)}, f32[128,16]{0,1:T(8,128)}, u32[]{:S(2)}) copy-start(f32[128,16]{0,1:T(8,128)} %param.14) | copy-start | bytes 24580
  125.9 0.7 copy-start.4
Sparse Core Ops, SparseCore 0:
  113.2 129.1 reduce-scatter.3
where the time goes:
time: 254 us; the launch traced here: 253 us
  blocking collectives  102 us (40%)
  waiting for transfers between devices  69.8 us (27%)
  local copies, waits for them, and re-layouts  22.9 us (9%)
  matrix products  20.6 us (8%)
  between operations  14.4 us (6%)
  starting transfers between devices  13.4 us (5%)
  other arithmetic  9.52 us (4%)
    psum x1, blocking collectives, on_device(): lax.psum((query_part, weight_part, gain_part), 'tok')  60.7 us
    unnamed x2, waiting for transfers between devices  48 us
    all_to_all x1, blocking collectives, on_device(): lax.all_to_all(returned, 'tok', split_axis=0, concat_axis=0, tiled=True)  30 us
    all_to_all x1, waiting for transfers between devices, on_device(): lax.all_to_all(row_blocks(five_view, blocks), 'tok', split_axis=0, concat...  21.7 us
    unnamed x25, local copies, waits for them, and re-layouts  16.6 us
    all_to_all x1, blocking collectives, on_device(): lax.all_to_all(grad_bias_part[None].astype(jnp.bfloat16), 'tok', split_ax...  11.2 us
    all_to_all x1, starting transfers between devices, on_device(): lax.all_to_all(dest_order(bias_wide), 'tok', split_axis=0, concat_axis=2,...  7.41 us
    all_to_all x1, starting transfers between devices, on_device(): lax.all_to_all(row_blocks(five_view, blocks), 'tok', split_axis=0, concat...  5.91 us
  transfers between devices with their start and end apart: 3, of which 3 were waited for; matrix products, arithmetic and copies ran while one was open for 6% of the time, Pallas kernels for 0%

commit v1 on v0

--- a/solution.py
+++ b/solution.py
@@ -167,8 +167,11 @@
     key_bias = (token_mask.astype(jnp.float32) - 1.0) * MASK_PENALTY
     joint_rows = jnp.concatenate([qkv_rows[:, :feature], gate, grad_gated], axis=1)
     bias_wide = jnp.broadcast_to(bias_cols[:, None], (HEADS, blocks) + bias_cols.shape[1:])
-    bias_full = lax.all_to_all(
-        dest_order(bias_wide), "tok", split_axis=0, concat_axis=2, tiled=True
+    bias_full = jnp.concatenate(
+        lax.all_to_all(
+            jnp.stack(jnp.split(dest_order(bias_wide), lax.axis_size("tok"), axis=0)), "tok", 0, 0
+        ),
+        axis=2,
     )[0].astype(jnp.float32)
     per_item = make_joint(bias_full, key_bias)
     five_rows = jnp.concatenate([joint_rows, qkv_rows[:, feature:]], axis=1)

time: 254 us -> 262 us (1.031)
  local copies, waits for them, and re-layouts: 22.9 us -> 31.6 us
    unnamed x25 -> x42, local copies, waits for them, and re-layouts: 16.6 us -> 25.3 us
where the time goes in v1:
time: 262 us; the launch traced here: 261 us
  blocking collectives  102 us (39%)
  waiting for transfers between devices  69.9 us (27%)
  local copies, waits for them, and re-layouts  31.6 us (12%)
  matrix products  20.5 us (8%)
  between operations  14.4 us (5%)
  starting transfers between devices  13.3 us (5%)
  other arithmetic  9.52 us (4%)
    psum x1, blocking collectives, on_device(): lax.psum((query_part, weight_part, gain_part), 'tok')  60.7 us
    unnamed x2, waiting for transfers between devices  48 us
    all_to_all x1, blocking collectives, on_device(): lax.all_to_all(returned, 'tok', split_axis=0, concat_axis=0, tiled=True)  30 us
    unnamed x42, local copies, waits for them, and re-layouts  25.3 us
    all_to_all x1, waiting for transfers between devices, on_device(): lax.all_to_all(row_blocks(five_view, blocks), 'tok', split_axis=0, concat...  21.7 us
    all_to_all x1, blocking collectives, on_device(): lax.all_to_all(grad_bias_part[None].astype(jnp.bfloat16), 'tok', split_ax...  11.2 us
    all_to_all x1, starting transfers between devices, on_device(): lax.all_to_all(jnp.stack(jnp.split(dest_order(bias_wide), lax.axis_size('...  7.41 us
    all_to_all x1, starting transfers between devices, on_device(): lax.all_to_all(row_blocks(five_view, blocks), 'tok', split_axis=0, concat...  5.8 us
  transfers between devices with their start and end apart: 3, of which 3 were waited for; matrix products, arithmetic and copies ran while one was open for 6% of the time, Pallas kernels for 0%

profile of v1, /device:TPU:0, one launch (start us, length us, event | category | flops | bytes accessed | tf_op | source)
XLA Modules:
  0.0 261.4 jit_solution(17716955801403759428)
XLA Ops:
  7.2 1.3 copy.440
  8.6 1.2 fusion.28
  9.9 0.6 constant_dynamic-update-slice_fusion.15
  10.5 0.6 constant_dynamic-update-slice_fusion.14
  11.1 0.6 constant_dynamic-update-slice_fusion.13
  11.6 0.6 constant_dynamic-update-slice_fusion.12
  12.2 0.6 constant_dynamic-update-slice_fusion.11
  12.8 0.6 constant_dynamic-update-slice_fusion.10
  13.4 0.6 constant_dynamic-update-slice_fusion.9
  14.0 0.6 constant_dynamic-update-slice_fusion.8
  14.5 0.6 constant_dynamic-update-slice_fusion.7
  15.1 0.6 constant_dynamic-update-slice_fusion.6
  15.7 0.6 constant_dynamic-update-slice_fusion.5
  16.3 0.6 constant_dynamic-update-slice_fusion.4
  16.9 0.6 constant_dynamic-update-slice_fusion.3
  17.4 0.6 constant_dynamic-update-slice_fusion.2
  18.0 0.6 constant_dynamic-update-slice_fusion.1
  18.6 0.6 constant_dynamic-update-slice_fusion
  19.2 7.4 %all-to-all-start.1 = ((bf16[16,1,128,8]{2,3,1,0:T(8,128)(2,1)}), bf16[16,1,128,8]{2,3,1,0:T(8,128)(2,1)S(1)}, u32[]{:S(2)}, u32[]{:S(2)}) async-start(bf16[16,1,128,8]{2,3,1,0:T(8,128)(2,1)} %constant_dynamic-update-slice_fusion), calls=%async_computation.1 | async-start | bytes 65536 | tf_op jit(solution)/shard_map/all_to_all | solution.py:171
  26.6 3.1 %fusion.58 = f32[128,3072]{1,0:T(8,128)S(1)} fusion(bf16[768,3072]{1,0:T(8,128)(2,1)} %param.15, bf16[1,128,768]{2,1,0:T(8,128)(2,1)S(1)} %copy-done.3), kind=kOutput, calls=%fused_computation.93 | convolution fusion | flops 603979776 | bytes 6488064 | tf_op jit(solution)/shard_map/dot_general | solution.py:151
  30.1 0.6 copy-done.1
  30.7 0.5 convolution_convert_fusion.3
  31.3 0.7 copy.438
  32.0 1.0 copy.439
  33.2 5.8 %all-to-all-start = ((bf16[16,5,48,128]{3,2,1,0:T(8,128)(2,1)}), bf16[16,5,48,128]{3,2,1,0:T(8,128)(2,1)S(1)}, u32[]{:S(2)}, u32[]{:S(2)}) async-start(bf16[16,5,48,128]{3,2,1,0:T(8,128)(2,1)} %copy.439), calls=%async_computation | async-start | bytes 1966080 | tf_op jit(solution)/shard_map/all_to_all | solution.py:179
  39.1 21.7 %all-to-all-done = bf16[16,5,48,128]{3,2,1,0:T(8,128)(2,1)S(1)} async-done(((bf16[16,5,48,128]{3,2,1,0:T(8,128)(2,1)}), bf16[16,5,48,128]{3,2,1,0:T(8,128)(2,1)S(1)}, u32[]{:S(2)}, u32[]{:S(2)}) %all-to-all-start) | async-done | bytes 983072 | tf_op jit(solution)/shard_map/all_to_all | solution.py:179
  60.9 10.9 %while.13 = (s32[]{:T(128)}, f32[128,128]{0,1:T(8,128)S(1)}, bf16[4,4,5,48,128]{4,3,2,1,0:T(8,128)(2,1)}, bf16[4,4,5,48,128]{4,3,2,1,0:T(8,128)(2,1)S(1)}, f32[1...) while((s32[]{:T(128)}, f32[128,128]{0,1:T(8,128)S(1)}, ...), condition=%wide.region_7.8_spmd.clone, body=%wide.region_2.7_spmd.clone.sunk | while | flops 52896640 | bytes 4685423 | solution.py:194
  62.9 0.7 copy_dynamic-update-slice_fusion.2
  65.6 0.7 copy_dynamic-update-slice_fusion.2
  68.3 0.7 copy_dynamic-update-slice_fusion.2
  71.1 0.7 copy_dynamic-update-slice_fusion.2
  71.8 30.0 %all_to_all.30 = bf16[16,5,48,128]{3,2,1,0:T(8,128)(2,1)S(1)} all-to-all(bf16[16,5,48,128]{3,2,1,0:T(8,128)(2,1)} %bitcast.249), channel_id=1, replica_groups=mesh['groups'=2,'tok'=16] {'tok'}, dimensions={0} | all-to-all | bytes 1966080 | tf_op jit(solution)/shard_map/all_to_all | solution.py:200
  101.9 0.8 copy-done.2
  102.7 0.5 fusion.53
  103.2 1.4 convolution_bitcast_fusion
  104.6 4.6 %pad_maximum_fusion = f32[768,3840]{0,1:T(8,128)} fusion(f32[768,768]{0,1:T(8,128)S(1)} %fusion.53, f32[768,3072]{0,1:T(8,128)S(1)} %convolution_bitcast_fusion), kind=kLoop, calls=%fused_computation.49 | loop fusion | flops 2949120 | bytes 23592960 | tf_op jit(solution)/shard_map/concatenate | solution.py:214
  109.2 12.4 %copy.458 = f32[768,3840]{1,0:T(8,128)} copy(f32[768,3840]{0,1:T(8,128)} %pad_maximum_fusion) | data formatting | bytes 23592960
  121.9 0.5 broadcast.94
  122.4 0.8 reduce
  123.3 11.2 %all_to_all.31 = bf16[16,2,512]{2,1,0:T(2,128)(2,1)S(1)} all-to-all(bf16[16,2,512]{2,1,0:T(2,128)(2,1)S(1)} %reshape.95), channel_id=1, replica_groups=mesh['groups'=2,'tok'=16] {'tok'}, dimensions={0} | all-to-all | bytes 65536 | tf_op jit(solution)/shard_map/all_to_all | solution.py:207
  134.6 0.6 fusion.41
  135.4 0.9 copy.449
  136.3 1.2 convolution_bitcast_fusion.1
  137.6 60.7 %all-reduce.1 = (f32[768]{0:T(1024)}, f32[128,16]{0,1:T(8,128)}, f32[128]{0:T(128)}) all-reduce(f32[768]{0:T(1024)S(1)} %convert_reduce_fusion.1, f32[128,16]{0,1:T(8,128)S(1)} %convolution_bitcast_fusion.1, f32[128]{0:T(128)S(1)} %get-tuple-element.304), channel_id=1, replica_groups=mesh['groups'=2,'tok'=16] {'tok'}, use_global_device_ids=true, to_apply=%region_12.13 | all-reduce | flops 2944 | bytes 23552 | tf_op jit(solution)/shard_map/psum | solution.py:223
  198.3 4.7 %fusion.27 = bf16[1,128,768]{2,1,0:T(8,128)(2,1)} fusion(bf16[768,3072]{1,0:T(8,128)(2,1)} %param.15, bf16[128,768]{0,1:T(8,128)(2,1)S(1)} %get-tuple-element.331, bf16[128,1536]{0,1:T(8,128)(2,1)S(1)} %slice.80, bf16[128,768]{0,1:T(8,128)(2,1)S(1)} %get-tuple-element.330), kind=kOutput, calls=%fused_computation.55 | convolution fusion | flops 606437376 | bytes 5701632 | tf_op jit(solution)/shard_map/rn,dn->rd/dot_general | solution.py:216
  203.0 48.0 %reduce-scatter.4.cloned.1.call-done = f32[48,3840]{1,0:T(8,128)} async-done(((f32[768,3840]{1,0:T(8,128)}), f32[48,3840]{1,0:T(8,128)}) %reduce-scatter.4.cloned.1.call-update) | async-done | bytes 737296
  251.0 1.6 slice.84
  252.6 1.9 slice.83
  (91 shorter events, 9.4 us)
Async XLA Ops:
  7.2 22.9 %copy-start = (bf16[768,768]{1,0:T(8,128)(2,1)S(1)}, bf16[768,768]{1,0:T(8,128)(2,1)}, u32[]{:S(2)}) copy-start(bf16[768,768]{1,0:T(8,128)(2,1)} %param.17) | copy-start | bytes 3538948
  7.2 19.4 %copy-start.3 = (bf16[1,128,768]{2,1,0:T(8,128)(2,1)S(1)}, bf16[1,128,768]{2,1,0:T(8,128)(2,1)}, u32[]{:S(2)}) copy-start(bf16[1,128,768]{2,1,0:T(8,128)(2,1)} %param.11) | copy-start | bytes 589828
  19.2 14.1 %all-to-all-start.1 = ((bf16[16,1,128,8]{2,3,1,0:T(8,128)(2,1)}), bf16[16,1,128,8]{2,3,1,0:T(8,128)(2,1)S(1)}, u32[]{:S(2)}, u32[]{:S(2)}) async-start(bf16[16,1,128,8]{2,3,1,0:T(8,128)(2,1)} %constant_dynamic-update-slice_fusion), calls=%async_computation.1 | async-start | bytes 65536 | tf_op jit(solution)/shard_map/all_to_all | solution.py:171
  26.6 3.3 %copy-start.6 = (f32[768]{0:T(1024)S(1)}, f32[768]{0:T(1024)}, u32[]{:S(2)}) copy-start(f32[768]{0:T(1024)} %param.16) | copy-start | bytes 9220
  29.7 0.9 copy-start.1
  32.0 7.2 %copy-start.9 = (s32[128]{0:T(128)S(1)}, s32[128]{0:T(128)}, u32[]{:S(2)}) copy-start(s32[128]{0:T(128)} %param.18) | copy-start | bytes 1540
  33.2 27.6 %all-to-all-start = ((bf16[16,5,48,128]{3,2,1,0:T(8,128)(2,1)}), bf16[16,5,48,128]{3,2,1,0:T(8,128)(2,1)S(1)}, u32[]{:S(2)}, u32[]{:S(2)}) async-start(bf16[16,5,48,128]{3,2,1,0:T(8,128)(2,1)} %copy.439), calls=%async_computation | async-start | bytes 1966080 | tf_op jit(solution)/shard_map/all_to_all | solution.py:179
  39.0 212.0 %reduce-scatter.4.cloned.1.call-start = ((), (), s32[]{:S(2)}) async-start(), calls=%async_computation.5 | async-start | bytes 12533760
  101.7 0.9 copy-start.2
  101.9 1.3 copy-start.4
  121.6 12.9 %copy-start.7 = (f32[128]{0:T(128)S(1)}, f32[128]{0:T(128)}, u32[]{:S(2)}) copy-start(f32[128]{0:T(128)} %param.13) | copy-start | bytes 1540
  121.6 12.9 %copy-start.8 = (f32[128,16]{0,1:T(8,128)S(1)}, f32[128,16]{0,1:T(8,128)}, u32[]{:S(2)}) copy-start(f32[128,16]{0,1:T(8,128)} %param.14) | copy-start | bytes 24580
  134.5 0.7 copy-start.5
Sparse Core Ops, SparseCore 0:
  121.8 129.1 reduce-scatter.3
